TPU v7x, 32 devices: a whole 2x2x4 slice. The times are simulated.
32 devices in a mesh: grp: 8 (over z, y), lane: 4 (over x, core).
Axes of the slice: x: 2, y: 2, z: 4, core: 2. Of those that a mesh axis runs over, the one named last changes fastest.
Arguments:
- grad_pooled: bfloat16 [4096, 16, 256], P(('grp', 'lane')), may hold values from -16 to 16
- bag_len: int32 [4096, 16], P(('grp', 'lane')), may hold values from 1 to 8
- lookup_slot: int32 [4096, 16, 8], P('grp', 'lane'), may hold values from -1 to 15, as said below
- slot_row: int32 [8, 4, 8, 2], P('grp', 'lane'), may hold values from 0 to 1023, as said below
- weights: float32 [16, 2048, 256], P('lane', 'grp'), may hold values from -6 to 6
- accum: float32 [16, 2048], P('lane', 'grp'), may hold values from 0.05 to 0.5
Outputs:
- new_weights: float32 [16, 2048, 256], P('lane', 'grp')
- new_accum: float32 [16, 2048], P('lane', 'grp')
Inputs may be any that keep to these rules, and one draw needn't show every extreme that they name: `lookup_slot`: position j of bag (b, t) holds -1 when j >= bag_len[b, t] and otherwise a slot number s; the row slot_row[s // 2, t // 4, g, s % 2], with g the group of sample b, lies in local table t % 4. `slot_row`: several slots, also from different groups, may name the same row.
All inputs are finite; a program needn't handle non-finite values.
Results may differ from a plain program's by a relative error of at most 0.0035.
Values may be sent and summed in bfloat16 or wider, within the bound.
A program may use at most 64 MiB of HBM per device.

v0:
```python
import math

import jax
import jax.numpy as jnp
from jax import lax
from jax.sharding import PartitionSpec as P

SLOTS_PEER = 2


LEARN_RATE = 0.3
EPSILON = 1e-06


def per_device(grad_pooled, bag_len, lookup_slot, slot_row, weights, accum):
    lane_count = lax.axis_size("lane")
    group_count = lax.axis_size("grp")
    number_slots = group_count * SLOTS_PEER
    batch_rows, table_count, embed_width = grad_pooled.shape
    tables_here = table_count // lane_count
    bag_depth = lookup_slot.shape[2]
    scaled = (grad_pooled.astype(jnp.float32) / bag_len.astype(jnp.float32)[:, :, None]).astype(
        jnp.bfloat16
    )
    own_slots = lax.all_to_all(lookup_slot, "lane", split_axis=0, concat_axis=1, tiled=True)
    slot_marks = jnp.transpose(
        own_slots.reshape(batch_rows, lane_count, tables_here, bag_depth), (1, 0, 2, 3)
    )
    numbers = lax.broadcasted_iota(jnp.int32, (1, number_slots, 1, 1, 1), 1)
    counts = jnp.sum(slot_marks[:, None] == numbers, axis=-1, dtype=jnp.int32).astype(jnp.bfloat16)
    values = scaled.reshape(batch_rows, lane_count, tables_here, embed_width)
    partial_here = jnp.einsum(
        "msbt,bmte->mse", counts, values, preferred_element_type=jnp.float32
    ).astype(jnp.bfloat16)
    partial_value = lax.all_to_all(partial_here, "lane", split_axis=0, concat_axis=0, tiled=True)
    slot_sum = jnp.sum(partial_value.astype(jnp.float32), axis=0).astype(jnp.bfloat16)
    outgoing = slot_sum.reshape(group_count, SLOTS_PEER, embed_width)
    incoming = lax.all_to_all(outgoing, "grp", split_axis=0, concat_axis=0, tiled=True).reshape(
        number_slots, embed_width
    )
    targets = slot_row.reshape(1, number_slots)
    local_rows = accum.shape[0] * accum.shape[1]
    row_ids = lax.broadcasted_iota(jnp.int32, (local_rows, 1), 0)
    placing = (row_ids == targets).astype(jnp.bfloat16)
    row_grad = jnp.dot(placing, incoming, preferred_element_type=jnp.float32)
    square_mean = jnp.mean(row_grad * row_grad, axis=1)
    norm_total = lax.psum(embed_width * jnp.sum(square_mean), ("grp", "lane"))
    clip_limit = 0.5 * math.sqrt(group_count * lane_count * number_slots * embed_width)
    clip_factor = clip_limit / jnp.maximum(jnp.sqrt(norm_total), clip_limit)
    new_accum = accum + clip_factor * clip_factor * square_mean.reshape(accum.shape)
    step_rows = LEARN_RATE * clip_factor * row_grad.reshape(weights.shape)
    new_weights = weights - step_rows / (jnp.sqrt(new_accum)[:, :, None] + EPSILON)
    return (new_weights, new_accum)


def solution(mesh):
    placed = (
        P(("grp", "lane"), None, None),
        P(("grp", "lane"), None),
        P("grp", "lane", None),
        P("grp", "lane", None, None),
        P("lane", "grp", None),
        P("lane", "grp"),
    )
    return jax.shard_map(
        per_device,
        mesh=mesh,
        in_specs=placed,
        out_specs=(P("lane", "grp", None), P("lane", "grp")),
        check_vma=False,
    )
```

profile of v0, /device:TPU:0, one launch (start us, length us, event | category | flops | bytes accessed | tf_op | source)
XLA Modules:
  0.0 79.0 jit_solution(7309163360748396572)
XLA Ops:
  0.6 0.0 copy-start.2
  0.6 0.0 copy-start
  0.6 1.3 %copy.21 = s32[512,4,8]{2,1,0:T(4,128)S(1)} copy(s32[512,4,8]{0,2,1:T(8,128)} %param.8) | data formatting | bytes 131072 | tf_op args[2]
  2.0 1.8 %reshape.32 = s32[4,1,4096]{2,1,0:T(1,128)} reshape(s32[512,4,8]{2,1,0:T(4,128)S(1)} %copy.21) | data formatting | bytes 131072
  3.7 4.2 %all-to-all-start = ((s32[4,1,4096]{2,1,0:T(1,128)}), s32[4,1,4096]{2,1,0:T(1,128)S(1)}, u32[]{:S(2)}, u32[]{:S(2)}) async-start(s32[4,1,4096]{2,1,0:T(1,128)} %reshape.32), calls=%async_computation | async-start | bytes 131072 | tf_op jit(solution)/shard_map/all_to_all | solution.py:25
  8.0 0.0 copy-done.2
  8.0 0.1 copy.23
  8.1 0.0 copy-done
  8.1 0.3 divide_convert_fusion
  8.4 0.4 copy.27
  8.8 3.3 %all-to-all-done = s32[4,1,4096]{2,1,0:T(1,128)S(1)} async-done(((s32[4,1,4096]{2,1,0:T(1,128)}), s32[4,1,4096]{2,1,0:T(1,128)S(1)}, u32[]{:S(2)}, u32[]{:S(2)}) %all-to-all-start) | async-done | bytes 65568 | tf_op jit(solution)/shard_map/all_to_all | solution.py:25
  12.1 0.5 broadcast.11
  12.6 0.8 %reduce.1 = s32[4,4096]{1,0:T(4,128)S(1)} reduce(s32[4,1,4096]{2,1,0:T(1,128)S(1)} %all-to-all-done, s32[]{:T(128)} %broadcast.11), dimensions={1}, to_apply=%all_to_all.15.reduce_sub_computation | reduce | bytes 131076 | tf_op jit(solution)/shard_map/all_to_all | solution.py:25
  13.4 1.3 %reshape.33 = s32[512,4,8]{2,1,0:T(4,128)S(1)} reshape(s32[4,4096]{1,0:T(4,128)S(1)} %reduce.1) | data formatting | bytes 131072
  14.7 0.3 copy.22
  15.0 0.0 copy-start.4
  15.0 0.4 convert_reduce_fusion
  15.4 0.0 copy-start.3
  15.4 0.2 fusion
  15.7 6.3 %all_to_all.22 = bf16[4,16,256]{2,1,0:T(8,128)(2,1)S(1)} all-to-all(bf16[4,16,256]{2,1,0:T(8,128)(2,1)S(1)} %fusion), channel_id=1, replica_groups=mesh['grp'=8,'lane'=4] {'lane'}, dimensions={0} | all-to-all | bytes 65536 | tf_op jit(solution)/shard_map/all_to_all | solution.py:35
  22.0 0.6 reshape.29
  22.6 6.3 %all-to-all-start.2 = ((bf16[8,2,256]{2,1,0:T(2,128)(2,1)}), bf16[8,2,256]{2,1,0:T(2,128)(2,1)S(1)}, u32[]{:S(2)}, u32[]{:S(2)}) async-start(bf16[8,2,256]{2,1,0:T(2,128)(2,1)} %reshape.29), calls=%async_computation.2 | async-start | bytes 16384 | tf_op jit(solution)/shard_map/all_to_all | solution.py:38
  28.9 0.0 copy-done.4
  28.9 0.1 copy.20
  29.0 0.1 eq.29
  29.1 6.4 %all-to-all-done.2 = bf16[8,2,256]{2,1,0:T(2,128)(2,1)S(1)} async-done(((bf16[8,2,256]{2,1,0:T(2,128)(2,1)}), bf16[8,2,256]{2,1,0:T(2,128)(2,1)S(1)}, u32[]{:S(2)}, u32[]{:S(2)}) %all-to-all-start.2) | async-done | bytes 8224 | tf_op jit(solution)/shard_map/all_to_all | solution.py:38
  35.4 0.4 multiply_reduce_fusion
  35.8 0.6 multiply_reduce_fusion.1
  37.1 38.2 %psum.7 = f32[]{:T(128)} all-reduce(f32[]{:T(128)S(6)} %mul.30), channel_id=1, replica_groups=mesh['grp'=8,'lane'=4] {'grp','lane'}, use_global_device_ids=true, to_apply=%region_4.0 | all-reduce | flops 1 | bytes 8 | tf_op jit(solution)/shard_map/psum | solution.py:47
  76.0 0.0 copy-done.3
  76.0 0.6 sqrt_add_fusion
  76.6 0.0 copy-start.1
  76.6 0.1 broadcast_multiply_fusion
  76.7 1.1 %copy-done.1 = f32[4,256,256]{2,1,0:T(8,128)S(1)} copy-done((f32[4,256,256]{2,1,0:T(8,128)S(1)}, f32[4,256,256]{2,1,0:T(8,128)}, u32[]{:S(2)}) %copy-start.1) | copy-done | bytes 1048600
  77.9 1.2 %divide_subtract_fusion = f32[4,256,256]{2,1,0:T(8,128)} fusion(f32[4,256,256]{2,1,0:T(8,128)S(1)} %copy-done.1, f32[4,256,256]{2,1,0:T(8,128)S(1)} %bitcast.12, f32[4,256]{1,0:T(4,128)S(1)} %get-tuple-element.2), kind=kLoop, calls=%fused_computation.3 | loop fusion | flops 524288 | bytes 3149824 | tf_op jit(solution)/shard_map/sub | solution.py:52
  (6 shorter events, 0.1 us)
Async XLA Ops:
  0.6 7.4 %copy-start.2 = (s32[128,16]{0,1:T(8,128)S(1)}, s32[128,16]{0,1:T(8,128)}, u32[]{:S(2)}) copy-start(s32[128,16]{0,1:T(8,128)} %param.7) | copy-start | bytes 24580
  0.6 7.5 %copy-start = (bf16[128,16,256]{2,1,0:T(8,128)(2,1)S(1)}, bf16[128,16,256]{2,1,0:T(8,128)(2,1)}, u32[]{:S(2)}) copy-start(bf16[128,16,256]{2,1,0:T(8,128)(2,1)} %param.6) | copy-start | bytes 3145732
  3.7 8.4 %all-to-all-start = ((s32[4,1,4096]{2,1,0:T(1,128)}), s32[4,1,4096]{2,1,0:T(1,128)S(1)}, u32[]{:S(2)}, u32[]{:S(2)}) async-start(s32[4,1,4096]{2,1,0:T(1,128)} %reshape.32), calls=%async_computation | async-start | bytes 131072 | tf_op jit(solution)/shard_map/all_to_all | solution.py:25
  15.0 13.9 %copy-start.4 = (s32[1,1,8,2]{2,3,1,0:T(2,128)S(1)}, s32[1,1,8,2]{2,3,1,0:T(2,128)}, u32[]{:S(2)}) copy-start(s32[1,1,8,2]{2,3,1,0:T(2,128)} %param.9) | copy-start | bytes 196
  15.4 60.6 %copy-start.3 = (f32[4,256]{1,0:T(4,128)S(1)}, f32[4,256]{1,0:T(4,128)}, u32[]{:S(2)}) copy-start(f32[4,256]{1,0:T(4,128)} %param.11) | copy-start | bytes 12292
  22.6 12.9 %all-to-all-start.2 = ((bf16[8,2,256]{2,1,0:T(2,128)(2,1)}), bf16[8,2,256]{2,1,0:T(2,128)(2,1)S(1)}, u32[]{:S(2)}, u32[]{:S(2)}) async-start(bf16[8,2,256]{2,1,0:T(2,128)(2,1)} %reshape.29), calls=%async_computation.2 | async-start | bytes 16384 | tf_op jit(solution)/shard_map/all_to_all | solution.py:38
  76.6 1.2 %copy-start.1 = (f32[4,256,256]{2,1,0:T(8,128)S(1)}, f32[4,256,256]{2,1,0:T(8,128)}, u32[]{:S(2)}) copy-start(f32[4,256,256]{2,1,0:T(8,128)} %param.10) | copy-start | bytes 3145732
where the time goes:
time: 79.6 us; the launch traced here: 79 us
  blocking collectives  44.5 us (56%)
  starting transfers between devices  10.6 us (13%)
  waiting for transfers between devices  9.65 us (12%)
  local copies, waits for them, and re-layouts  7.56 us (9%)
  other arithmetic  4.03 us (5%)
  between operations  2.13 us (3%)
    psum x1, blocking collectives, per_device(): norm_total = lax.psum(embed_width * jnp.sum(square_mean), ('grp', 'lane'))  38.2 us
    all_to_all x1, waiting for transfers between devices, per_device(): lax.all_to_all(outgoing, 'grp', split_axis=0, concat_axis=0, tiled=True)  6.35 us
    all_to_all x1, starting transfers between devices, per_device(): lax.all_to_all(outgoing, 'grp', split_axis=0, concat_axis=0, tiled=True)  6.33 us
    all_to_all x1, blocking collectives, per_device(): lax.all_to_all(partial_here, 'lane', split_axis=0, concat_axis=0, tiled=T...  6.3 us
    unnamed x14, local copies, waits for them, and re-layouts  5.6 us
    all_to_all x1, starting transfers between devices, per_device(): lax.all_to_all(lookup_slot, 'lane', split_axis=0, concat_axis=1, tiled=True)  4.24 us
    all_to_all x1, waiting for transfers between devices, per_device(): lax.all_to_all(lookup_slot, 'lane', split_axis=0, concat_axis=1, tiled=True)  3.3 us
  transfers between devices with their start and end apart: 2, of which 2 were waited for; matrix products, arithmetic and copies ran while one was open for 1% of the time, Pallas kernels for 0%

commit v1 on v0

v1 whole, which is shorter than its diff:
```python
import functools
import math

import jax
import jax.numpy as jnp
from jax import lax
from jax.experimental import pallas as pl
from jax.experimental.pallas import tpu as pltpu
from jax.sharding import PartitionSpec as P

MESH = pl.DeviceIdType.MESH
LEARN_RATE = 0.3
EPSILON = 1e-06
F32 = jnp.float32
BF16 = jnp.bfloat16


def each(count, body):
    if count <= 64:
        for i in range(count):
            body(i)
    else:

        def step(i, carry):
            body(i)
            return carry

        lax.fori_loop(0, count, step, 0)


def iota(shape, dim):
    return lax.broadcasted_iota(jnp.int32, shape, dim)


def kernel(
    groups,
    lanes,
    grad_hbm,
    len_hbm,
    look_hbm,
    slot_hbm,
    weights_hbm,
    accum_hbm,
    wout,
    aout,
    grad_in,
    grad_f32,
    grad_t,
    len_v,
    marks,
    marks_out,
    slot_v,
    accum_v,
    part,
    recv,
    incoming,
    norm_out,
    norm_in,
    load_sem,
    look_sem,
    a_send,
    a_recv,
    b_send,
    b_recv,
    c_send,
    c_recv,
):
    devices = groups * lanes
    per_peer, embed = recv.shape[1], recv.shape[2]
    slots = groups * per_peer
    tables_all, batch = grad_t.shape[0], grad_t.shape[1]
    tables = tables_all // lanes
    depth = marks.shape[2]
    rows = accum_v.shape[1]
    grp = lax.axis_index("grp")
    lane = lax.axis_index("lane")
    me = grp * lanes + lane

    lane_steps = [(dx, dc) for dx in range(lanes // 2) for dc in range(2)]

    def lane_peer(step, sign):
        dx, dc = step
        half = lanes // 2
        chip = (lane // 2 + sign * dx + half) % half
        return chip * 2 + (lane % 2 + dc) % 2

    barrier = pltpu.get_barrier_semaphore()

    def greet(i):
        far = (me + i + 1) % devices
        pl.semaphore_signal(
            barrier, inc=1, device_id=(far // lanes, far % lanes), device_id_type=MESH
        )

    look_copies = []
    for k, step in enumerate(lane_steps):
        q = lane_peer(step, 1)
        src = look_hbm.at[:, :, pl.ds(pl.multiple_of(q * batch, batch), batch)]
        dst = marks.at[lane] if k == 0 else marks_out.at[k - 1]
        look_copies.append(pltpu.make_async_copy(src, dst, look_sem.at[k]))
        look_copies[-1].start()
    grad_copy = pltpu.make_async_copy(grad_hbm, grad_in, load_sem.at[0])
    grad_copy.start()
    each(devices - 1, greet)
    small_copies = [
        pltpu.make_async_copy(len_hbm, len_v, load_sem.at[1]),
        pltpu.make_async_copy(slot_hbm, slot_v, load_sem.at[2]),
        pltpu.make_async_copy(accum_hbm, accum_v, load_sem.at[3]),
        pltpu.make_async_copy(weights_hbm, wout, load_sem.at[4]),
    ]
    for copy in small_copies:
        copy.start()
    for copy in look_copies:
        copy.wait()
    pl.semaphore_wait(barrier, devices - 1)

    a_copies = []
    for k, step in enumerate(lane_steps[1:], 1):
        copy = pltpu.make_async_remote_copy(
            src_ref=marks_out.at[k - 1],
            dst_ref=marks.at[lane],
            send_sem=a_send.at[k - 1],
            recv_sem=a_recv.at[k - 1],
            device_id=(grp, lane_peer(step, 1)),
            device_id_type=MESH,
        )
        copy.start()
        a_copies.append(copy)

    grad_copy.wait()
    for c in range(embed // 128):
        grad_f32[c] = grad_in[:, c * 128 : (c + 1) * 128].astype(F32)
    for t in range(tables_all):
        for c in range(embed // 128):
            grad_t[t, :, c * 128 : (c + 1) * 128] = grad_f32[
                c, pl.ds(t, batch, stride=tables_all), :
            ].astype(BF16)
    for copy in small_copies[:3]:
        copy.wait()

    number = iota((slots, batch), 0)
    far_first = sorted(range(groups), key=lambda d: abs(d - groups // 2))

    for k, step in enumerate(lane_steps):
        m = lane_peer(step, -1)
        if k > 0:
            a_copies[k - 1].wait_recv()
        highs, lows = [], []
        for t in range(tables):
            mark = marks[m, t]
            count = jnp.zeros((slots, batch), F32)
            for j in range(depth):
                count += jnp.where(mark[j : j + 1, :] == number, 1.0, 0.0)
            length = len_v[pl.ds(m * tables + t, 1), :].astype(F32)
            factor = count / length
            high = factor.astype(BF16)
            highs.append(high)
            lows.append((factor - high.astype(F32)).astype(BF16))
        factors = jnp.concatenate(
            [jnp.concatenate(highs, axis=1), jnp.concatenate(lows, axis=1)], axis=0
        )
        values = grad_t[pl.ds(m * tables, tables)].reshape(tables * batch, embed)
        both = jnp.dot(factors, values, preferred_element_type=F32)
        total = both[:slots] + both[slots:]
        for p in range(groups):
            part[m, p] = total[p * per_peer : (p + 1) * per_peer].astype(BF16)

        def send(p):
            pltpu.make_async_remote_copy(
                src_ref=part.at[m, p],
                dst_ref=recv.at[me],
                send_sem=b_send,
                recv_sem=b_recv,
                device_id=(p, m),
                device_id_type=MESH,
            ).start()

        if groups <= 64:
            for dp in far_first:
                if k == 0 and dp == 0:
                    pltpu.make_async_copy(part.at[m, grp], recv.at[me], b_recv).start()
                else:
                    send((grp + dp) % groups)
        else:
            each(groups - 1, lambda i: send((grp + i + 1) % groups))
            if k == 0:
                pltpu.make_async_copy(part.at[m, grp], recv.at[me], b_recv).start()
            else:
                send(grp)

    slot_f = slot_v[...].astype(F32)
    which = iota((slots, groups), 0)
    column_pick = jnp.zeros((slots, groups), F32)
    for k in range(per_peer):
        column_pick = jnp.where(which % per_peer == k, slot_f[k : k + 1, :], column_pick)
    column_pick = jnp.where(which // per_peer == iota((slots, groups), 1), column_pick, 0.0)
    target_col = jnp.sum(column_pick, axis=1, keepdims=True)
    i_id, j_id = iota((slots, slots), 0), iota((slots, slots), 1)
    target_row = jnp.sum(jnp.where(i_id == j_id, target_col, 0.0), axis=0, keepdims=True)
    same = target_col == target_row
    first_col = jnp.sum(jnp.where(same & (j_id < i_id), 1.0, 0.0), axis=1, keepdims=True) == 0.0
    first_row = jnp.sum(jnp.where(same & (i_id < j_id), 1.0, 0.0), axis=0, keepdims=True) == 0.0
    place_row = jnp.where(first_row, target_row, -1.0)
    place_row = jnp.concatenate([place_row, place_row], axis=1)
    same_w = jnp.where(same, 1.0, 0.0).astype(BF16)

    hits = []
    accum_col = jnp.zeros((slots, 1), F32)
    for t in range(tables):
        hit = target_col == (iota((slots, rows), 1) + t * rows).astype(F32)
        hits.append(hit)
        accum_col += jnp.sum(
            jnp.where(hit, accum_v[t : t + 1, :], 0.0), axis=1, keepdims=True
        )

    pltpu.make_async_copy(recv, recv, b_recv).wait()
    for g in range(groups):
        group_sum = recv[g * lanes].astype(F32)
        for q in range(1, lanes):
            group_sum += recv[g * lanes + q].astype(F32)
        incoming[g * per_peer : (g + 1) * per_peer, :] = group_sum
    grads = jnp.dot(same_w, incoming[...].astype(BF16), preferred_element_type=F32)
    square_col = jnp.sum(grads * grads, axis=1, keepdims=True) * (1.0 / embed)
    square_first = jnp.where(first_col, square_col, 0.0)
    local = embed * jnp.sum(square_first, axis=0, keepdims=True)
    norm_out[...] = jnp.broadcast_to(local, (1, 128))

    def tell(far):
        pltpu.make_async_remote_copy(
            src_ref=norm_out,
            dst_ref=norm_in.at[me],
            send_sem=c_send,
            recv_sem=c_recv,
            device_id=(far // lanes, far % lanes),
            device_id_type=MESH,
        ).start()

    if devices <= 64:
        for d in sorted(range(1, devices), key=lambda d: abs(d - devices // 2)):
            tell((me + d) % devices)
    else:
        each(devices - 1, lambda i: tell((me + i + 1) % devices))
    pltpu.make_async_copy(norm_out, norm_in.at[me], c_recv).start()

    square_rows = [
        jnp.sum(jnp.where(hit, square_first, 0.0), axis=0, keepdims=True) for hit in hits
    ]
    for copy in a_copies:
        copy.wait_send()
    small_copies[3].wait()
    sent = recv.at[pl.ds(0, devices - 1)]
    pltpu.make_async_copy(sent, sent, b_send).wait()

    pltpu.make_async_copy(norm_in, norm_in, c_recv).wait()
    norm_total = jnp.sum(norm_in[...], axis=0)[:, :1]
    clip_limit = 0.5 * math.sqrt(devices * slots * embed)
    clip = clip_limit / jnp.maximum(jnp.sqrt(norm_total), clip_limit)
    for t in range(tables):
        aout[t : t + 1, :] = accum_v[t : t + 1, :] + clip * clip * square_rows[t]
    new_accum_col = accum_col + clip * clip * square_col
    delta = LEARN_RATE * clip * grads / (jnp.sqrt(new_accum_col) + EPSILON)
    delta_high = delta.astype(BF16)
    delta_low = (delta - delta_high.astype(F32)).astype(BF16)
    deltas = jnp.concatenate([delta_high, delta_low], axis=0)
    for t in range(tables):
        row_id = (iota((rows, 1), 0) + t * rows).astype(F32)
        place = jnp.where(row_id == place_row, 1.0, 0.0).astype(BF16)
        wout[t] = wout[t] - jnp.dot(place, deltas, preferred_element_type=F32)
    told = norm_in.at[pl.ds(0, devices - 1)]
    pltpu.make_async_copy(told, told, c_send).wait()


def per_device(groups, lanes, grad_pooled, bag_len, lookup_slot, slot_row, weights, accum):
    batch, tables_all, embed = grad_pooled.shape
    samples, tables, depth = lookup_slot.shape
    rows = accum.shape[1]
    per_peer = slot_row.shape[3]
    devices = groups * lanes
    slots = groups * per_peer
    anywhere = pl.BlockSpec(memory_space=pl.ANY)
    vmem = pl.BlockSpec(memory_space=pltpu.VMEM)
    return pl.pallas_call(
        functools.partial(kernel, groups, lanes),
        out_shape=(
            jax.ShapeDtypeStruct(weights.shape, F32),
            jax.ShapeDtypeStruct(accum.shape, F32),
        ),
        in_specs=[anywhere] * 6,
        out_specs=(vmem, vmem),
        scratch_shapes=[
            pltpu.VMEM((batch * tables_all, embed), BF16),
            pltpu.VMEM((embed // 128, batch * tables_all, 128), F32),
            pltpu.VMEM((tables_all, batch, embed), BF16),
            pltpu.VMEM((tables_all, batch), jnp.int32),
            pltpu.VMEM((lanes, tables, depth, batch), jnp.int32),
            pltpu.VMEM((lanes - 1, tables, depth, batch), jnp.int32),
            pltpu.VMEM((per_peer, groups), jnp.int32),
            pltpu.VMEM((tables, rows), F32),
            pltpu.VMEM((lanes, groups, per_peer, embed), BF16),
            pltpu.VMEM((devices, per_peer, embed), BF16),
            pltpu.VMEM((slots, embed), F32),
            pltpu.VMEM((1, 128), F32),
            pltpu.VMEM((devices, 1, 128), F32),
            pltpu.SemaphoreType.DMA((5,)),
            pltpu.SemaphoreType.DMA((lanes,)),
            pltpu.SemaphoreType.DMA((lanes - 1,)),
            pltpu.SemaphoreType.DMA((lanes - 1,)),
            pltpu.SemaphoreType.DMA,
            pltpu.SemaphoreType.DMA,
            pltpu.SemaphoreType.DMA,
            pltpu.SemaphoreType.DMA,
        ],
        compiler_params=pltpu.CompilerParams(collective_id=0, has_side_effects=True),
    )(
        grad_pooled.reshape(batch * tables_all, embed),
        bag_len.T,
        jnp.transpose(lookup_slot, (1, 2, 0)),
        slot_row.reshape(groups, per_peer).T,
        weights,
        accum,
    )


def solution(mesh):
    placed = (
        P(("grp", "lane"), None, None),
        P(("grp", "lane"), None),
        P("grp", "lane", None),
        P("grp", "lane", None, None),
        P("lane", "grp", None),
        P("lane", "grp"),
    )
    return jax.shard_map(
        functools.partial(per_device, mesh.shape["grp"], mesh.shape["lane"]),
        mesh=mesh,
        in_specs=placed,
        out_specs=(P("lane", "grp", None), P("lane", "grp")),
        check_vma=False,
    )
```

time: 79.6 us -> 23.9 us (0.30)
  blocking collectives: 44.5 us -> 0 us
  Pallas kernels: 0 us -> 20.2 us
  starting transfers between devices: 10.6 us -> 0 us
  waiting for transfers between devices: 9.65 us -> 0 us
  local copies, waits for them, and re-layouts: 7.56 us -> 2.88 us
  other arithmetic: 4.03 us -> 0 us
  between operations: 2.13 us -> 0.65 us
    psum x1 -> x0, blocking collectives: 38.2 us -> none  [per_device(): norm_total = lax.psum(embed_width * jnp.sum(square_mean), ('grp', 'lane'))]
    pallas_call x0 -> x1, Pallas kernels: none -> 20.2 us  [per_device(): pl.pallas_call(functools.partial(kernel, groups, lanes), out_shape=(jax.S...]
    all_to_all x2 -> x0, starting transfers between devices: 10.6 us -> none  [the longest x1 6.33 us: per_device(): lax.all_to_all(outgoing, 'grp', split_axis=0, concat_axis=0, tiled=True)]
    all_to_all x2 -> x0, waiting for transfers between devices: 9.65 us -> none  [the longest x1 6.35 us: per_device(): lax.all_to_all(outgoing, 'grp', split_axis=0, concat_axis=0, tiled=True)]
    all_to_all x1 -> x0, blocking collectives: 6.3 us -> none  [per_device(): lax.all_to_all(partial_here, 'lane', split_axis=0, concat_axis=0, tiled=T...]
    unnamed x14 -> x4, local copies, waits for them, and re-layouts: 5.6 us -> 2.88 us
    sub x1 -> x0, other arithmetic: 1.18 us -> none  [per_device(): weights - step_rows / (jnp.sqrt(new_accum)[:, :, None] + EPSILON)]
    reduce_sum x3 -> x0, other arithmetic: 1 us -> none  [the longest x1 0.61 us: per_device(): norm_total = lax.psum(embed_width * jnp.sum(square_mean), ('grp', 'lane'))]
  transfers between devices with their start and end apart: 2 -> 0, of which waited for: 2 -> 0; matrix products, arithmetic and copies ran while one was open for 1% -> 0% of each run, Pallas kernels for 0% -> 0%
where the time goes in v1:
time: 23.9 us; the launch traced here: 23.8 us
  Pallas kernels  20.2 us (85%)
  local copies, waits for them, and re-layouts  2.88 us (12%)
  between operations  0.65 us (3%)
    pallas_call x1, Pallas kernels, per_device(): pl.pallas_call(functools.partial(kernel, groups, lanes), out_shape=(jax.S...  20.2 us
    unnamed x4, local copies, waits for them, and re-layouts  2.88 us

profile of v1, /device:TPU:0, one launch (start us, length us, event | category | flops | bytes accessed | tf_op | source)
XLA Modules:
  0.0 23.8 jit_solution(17047849041036285883)
XLA Ops:
  0.6 20.2 %shard_map.77 = (f32[4,256,256]{2,1,0:T(8,128)}, f32[4,256]{1,0:T(4,128)}) custom-call(bf16[2048,256]{1,0:T(8,128)(2,1)} %bitcast.6, s32[16,128]{1,0:T(8,128)} %bitcast.8, s32[4,8,512]{2,1,0:T(8,128)} %bitcast.7, s32[2,8]{1,0:T(2,128)} %bitcast.9, f32[4,256,256]{2,1,0:T(8,128)} %weights_hbm.1, f32[4,256]{1,0:T(4,128)} %accum_hbm.1), custom_call_target="tpu_custom_call" | custom-call | tf_op jit(solution)/shard_map/pallas_call | solution.py:282
  20.9 0.0 copy-start
  20.9 2.3 %copy.10 = f32[4,256,256]{2,1,0:T(8,128)} copy(f32[4,256,256]{2,1,0:T(8,128)} %get-tuple-element.4) | data formatting | bytes 2097152
  23.2 0.0 copy-done
  23.2 0.6 %copy.11 = f32[4,256]{1,0:T(4,128)} copy(f32[4,256]{1,0:T(4,128)S(1)} %copy-done) | data formatting | bytes 8192
Async XLA Ops:
  20.9 2.3 %copy-start = (f32[4,256]{1,0:T(4,128)S(1)}, f32[4,256]{1,0:T(4,128)}, u32[]{:S(2)}) copy-start(f32[4,256]{1,0:T(4,128)} %get-tuple-element.5) | copy-start | bytes 12292

commit v2 on v1

--- a/solution.py
+++ b/solution.py
@@ -39,9 +39,9 @@
     len_hbm,
     look_hbm,
     slot_hbm,
-    weights_hbm,
     accum_hbm,
-    wout,
+    delta_out,
+    place_out,
     aout,
     grad_in,
     grad_f32,
@@ -84,67 +84,7 @@
         chip = (lane // 2 + sign * dx + half) % half
         return chip * 2 + (lane % 2 + dc) % 2
 
-    barrier = pltpu.get_barrier_semaphore()
-
-    def greet(i):
-        far = (me + i + 1) % devices
-        pl.semaphore_signal(
-            barrier, inc=1, device_id=(far // lanes, far % lanes), device_id_type=MESH
-        )
-
-    look_copies = []
-    for k, step in enumerate(lane_steps):
-        q = lane_peer(step, 1)
-        src = look_hbm.at[:, :, pl.ds(pl.multiple_of(q * batch, batch), batch)]
-        dst = marks.at[lane] if k == 0 else marks_out.at[k - 1]
-        look_copies.append(pltpu.make_async_copy(src, dst, look_sem.at[k]))
-        look_copies[-1].start()
-    grad_copy = pltpu.make_async_copy(grad_hbm, grad_in, load_sem.at[0])
-    grad_copy.start()
-    each(devices - 1, greet)
-    small_copies = [
-        pltpu.make_async_copy(len_hbm, len_v, load_sem.at[1]),
-        pltpu.make_async_copy(slot_hbm, slot_v, load_sem.at[2]),
-        pltpu.make_async_copy(accum_hbm, accum_v, load_sem.at[3]),
-        pltpu.make_async_copy(weights_hbm, wout, load_sem.at[4]),
-    ]
-    for copy in small_copies:
-        copy.start()
-    for copy in look_copies:
-        copy.wait()
-    pl.semaphore_wait(barrier, devices - 1)
-
-    a_copies = []
-    for k, step in enumerate(lane_steps[1:], 1):
-        copy = pltpu.make_async_remote_copy(
-            src_ref=marks_out.at[k - 1],
-            dst_ref=marks.at[lane],
-            send_sem=a_send.at[k - 1],
-            recv_sem=a_recv.at[k - 1],
-            device_id=(grp, lane_peer(step, 1)),
-            device_id_type=MESH,
-        )
-        copy.start()
-        a_copies.append(copy)
-
-    grad_copy.wait()
-    for c in range(embed // 128):
-        grad_f32[c] = grad_in[:, c * 128 : (c + 1) * 128].astype(F32)
-    for t in range(tables_all):
-        for c in range(embed // 128):
-            grad_t[t, :, c * 128 : (c + 1) * 128] = grad_f32[
-                c, pl.ds(t, batch, stride=tables_all), :
-            ].astype(BF16)
-    for copy in small_copies[:3]:
-        copy.wait()
-
-    number = iota((slots, batch), 0)
-    far_first = sorted(range(groups), key=lambda d: abs(d - groups // 2))
-
-    for k, step in enumerate(lane_steps):
-        m = lane_peer(step, -1)
-        if k > 0:
-            a_copies[k - 1].wait_recv()
+    def partial_of(m):
         highs, lows = [], []
         for t in range(tables):
             mark = marks[m, t]
@@ -161,7 +101,74 @@
         )
         values = grad_t[pl.ds(m * tables, tables)].reshape(tables * batch, embed)
         both = jnp.dot(factors, values, preferred_element_type=F32)
-        total = both[:slots] + both[slots:]
+        return both[:slots] + both[slots:]
+
+    barrier = pltpu.get_barrier_semaphore()
+
+    def greet(i):
+        far = (me + i + 1) % devices
+        pl.semaphore_signal(
+            barrier, inc=1, device_id=(far // lanes, far % lanes), device_id_type=MESH
+        )
+
+    if devices <= 64:
+        for i in sorted(range(devices - 1), key=lambda i: abs(i + 1 - devices // 2)):
+            greet(i)
+    else:
+        each(devices - 1, greet)
+    look_copies = []
+    for k, step in enumerate(lane_steps):
+        q = lane_peer(step, 1)
+        src = look_hbm.at[:, :, pl.ds(pl.multiple_of(q * batch, batch), batch)]
+        dst = marks.at[lane] if k == 0 else marks_out.at[k - 1]
+        look_copies.append(pltpu.make_async_copy(src, dst, look_sem.at[k]))
+        look_copies[-1].start()
+    grad_copy = pltpu.make_async_copy(grad_hbm, grad_in, load_sem.at[0])
+    grad_copy.start()
+    small_copies = [
+        pltpu.make_async_copy(len_hbm, len_v, load_sem.at[1]),
+        pltpu.make_async_copy(slot_hbm, slot_v, load_sem.at[2]),
+        pltpu.make_async_copy(accum_hbm, accum_v, load_sem.at[3]),
+    ]
+    for copy in small_copies:
+        copy.start()
+    for copy in look_copies:
+        copy.wait()
+    grad_copy.wait()
+    for c in range(embed // 128):
+        grad_f32[c] = grad_in[:, c * 128 : (c + 1) * 128].astype(F32)
+    for t in range(tables_all):
+        for c in range(embed // 128):
+            grad_t[t, :, c * 128 : (c + 1) * 128] = grad_f32[
+                c, pl.ds(t, batch, stride=tables_all), :
+            ].astype(BF16)
+    for copy in small_copies:
+        copy.wait()
+
+    number = iota((slots, batch), 0)
+    own_part = partial_of(lane)
+    pl.semaphore_wait(barrier, devices - 1)
+
+    a_copies = []
+    for k, step in enumerate(lane_steps[1:], 1):
+        copy = pltpu.make_async_remote_copy(
+            src_ref=marks_out.at[k - 1],
+            dst_ref=marks.at[lane],
+            send_sem=a_send.at[k - 1],
+            recv_sem=a_recv.at[k - 1],
+            device_id=(grp, lane_peer(step, 1)),
+            device_id_type=MESH,
+        )
+        copy.start()
+        a_copies.append(copy)
+
+    far_first = sorted(range(groups), key=lambda d: abs(d - groups // 2))
+
+    for k, step in enumerate(lane_steps):
+        m = lane_peer(step, -1)
+        if k > 0:
+            a_copies[k - 1].wait_recv()
+        total = own_part if k == 0 else partial_of(m)
         for p in range(groups):
             part[m, p] = total[p * per_peer : (p + 1) * per_peer].astype(BF16)
 
@@ -201,7 +208,7 @@
     first_col = jnp.sum(jnp.where(same & (j_id < i_id), 1.0, 0.0), axis=1, keepdims=True) == 0.0
     first_row = jnp.sum(jnp.where(same & (i_id < j_id), 1.0, 0.0), axis=0, keepdims=True) == 0.0
     place_row = jnp.where(first_row, target_row, -1.0)
-    place_row = jnp.concatenate([place_row, place_row], axis=1)
+    place_out[...] = jnp.concatenate([place_row, place_row], axis=1)
     same_w = jnp.where(same, 1.0, 0.0).astype(BF16)
 
     hits = []
@@ -247,7 +254,6 @@
     ]
     for copy in a_copies:
         copy.wait_send()
-    small_copies[3].wait()
     sent = recv.at[pl.ds(0, devices - 1)]
     pltpu.make_async_copy(sent, sent, b_send).wait()
 
@@ -260,14 +266,59 @@
     new_accum_col = accum_col + clip * clip * square_col
     delta = LEARN_RATE * clip * grads / (jnp.sqrt(new_accum_col) + EPSILON)
     delta_high = delta.astype(BF16)
-    delta_low = (delta - delta_high.astype(F32)).astype(BF16)
-    deltas = jnp.concatenate([delta_high, delta_low], axis=0)
-    for t in range(tables):
-        row_id = (iota((rows, 1), 0) + t * rows).astype(F32)
-        place = jnp.where(row_id == place_row, 1.0, 0.0).astype(BF16)
-        wout[t] = wout[t] - jnp.dot(place, deltas, preferred_element_type=F32)
+    delta_out[:slots] = delta_high
+    delta_out[slots:] = (delta - delta_high.astype(F32)).astype(BF16)
     told = norm_in.at[pl.ds(0, devices - 1)]
     pltpu.make_async_copy(told, told, c_send).wait()
+
+
+def update_kernel(
+    chunk,
+    weights,
+    delta_any,
+    place_any,
+    accum_any,
+    wout,
+    aout,
+    held,
+    delta,
+    place_row,
+    accum,
+    sems,
+    in_sems,
+    accum_sem,
+):
+    loads = [
+        pltpu.make_async_copy(place_any, place_row, in_sems.at[0]),
+        pltpu.make_async_copy(delta_any, delta, in_sems.at[1]),
+        pltpu.make_async_copy(accum_any, accum, in_sems.at[2]),
+    ]
+    for copy in loads:
+        copy.start()
+    for copy in loads:
+        copy.wait()
+    accum_copy = pltpu.make_async_copy(accum, aout, accum_sem)
+    accum_copy.start()
+    tables, rows = weights.shape[0], weights.shape[1]
+    copies = []
+    for t in range(tables):
+        for c in range(0, rows, chunk):
+            row_id = (iota((chunk, 1), 0) + (t * rows + c)).astype(F32)
+            place = jnp.where(row_id == place_row[...], 1.0, 0.0).astype(BF16)
+            held[t, c : c + chunk] = weights[t, c : c + chunk] - jnp.dot(
+                place, delta[...], preferred_element_type=F32
+            )
+            copies.append(
+                pltpu.make_async_copy(
+                    held.at[t, pl.ds(c, chunk)],
+                    wout.at[t, pl.ds(c, chunk)],
+                    sems.at[len(copies)],
+                )
+            )
+            copies[-1].start()
+    for copy in copies:
+        copy.wait()
+    accum_copy.wait()
 
 
 def per_device(groups, lanes, grad_pooled, bag_len, lookup_slot, slot_row, weights, accum):
@@ -279,14 +330,20 @@
     slots = groups * per_peer
     anywhere = pl.BlockSpec(memory_space=pl.ANY)
     vmem = pl.BlockSpec(memory_space=pltpu.VMEM)
-    return pl.pallas_call(
+    delta, place_row, accum_new = pl.pallas_call(
         functools.partial(kernel, groups, lanes),
         out_shape=(
-            jax.ShapeDtypeStruct(weights.shape, F32),
+            jax.ShapeDtypeStruct((2 * slots, embed), BF16),
+            jax.ShapeDtypeStruct((1, 2 * slots), F32),
             jax.ShapeDtypeStruct(accum.shape, F32),
         ),
-        in_specs=[anywhere] * 6,
-        out_specs=(vmem, vmem),
+        in_specs=[pl.BlockSpec(memory_space=pltpu.HBM)] * 5,
+        out_specs=(vmem, vmem, vmem),
+        cost_estimate=pl.CostEstimate(
+            flops=8 * slots * batch * tables_all * embed,
+            bytes_accessed=32 * batch * tables_all * embed,
+            transcendentals=0,
+        ),
         scratch_shapes=[
             pltpu.VMEM((batch * tables_all, embed), BF16),
             pltpu.VMEM((embed // 128, batch * tables_all, 128), F32),
@@ -301,7 +358,7 @@
             pltpu.VMEM((slots, embed), F32),
             pltpu.VMEM((1, 128), F32),
             pltpu.VMEM((devices, 1, 128), F32),
-            pltpu.SemaphoreType.DMA((5,)),
+            pltpu.SemaphoreType.DMA((4,)),
             pltpu.SemaphoreType.DMA((lanes,)),
             pltpu.SemaphoreType.DMA((lanes - 1,)),
             pltpu.SemaphoreType.DMA((lanes - 1,)),
@@ -310,15 +367,36 @@
             pltpu.SemaphoreType.DMA,
             pltpu.SemaphoreType.DMA,
         ],
-        compiler_params=pltpu.CompilerParams(collective_id=0, has_side_effects=True),
+        compiler_params=pltpu.CompilerParams(
+            collective_id=0, has_side_effects=True
+        ),
     )(
         grad_pooled.reshape(batch * tables_all, embed),
         bag_len.T,
         jnp.transpose(lookup_slot, (1, 2, 0)),
         slot_row.reshape(groups, per_peer).T,
-        weights,
         accum,
     )
+    chunk = min(rows, 128)
+    return pl.pallas_call(
+        functools.partial(update_kernel, chunk),
+        out_shape=(
+            jax.ShapeDtypeStruct(weights.shape, F32),
+            jax.ShapeDtypeStruct(accum.shape, F32),
+        ),
+        in_specs=[vmem, anywhere, anywhere, anywhere],
+        out_specs=(anywhere, anywhere),
+        scratch_shapes=[
+            pltpu.VMEM(weights.shape, F32),
+            pltpu.VMEM(delta.shape, BF16),
+            pltpu.VMEM(place_row.shape, F32),
+            pltpu.VMEM(accum.shape, F32),
+            pltpu.SemaphoreType.DMA((tables * (rows // chunk),)),
+            pltpu.SemaphoreType.DMA((3,)),
+            pltpu.SemaphoreType.DMA,
+        ],
+        compiler_params=pltpu.CompilerParams(vmem_limit_bytes=8 << 20),
+    )(weights, delta, place_row, accum_new)
 
 
 def solution(mesh):

time: 23.9 us -> 23.5 us (0.983)
  local copies, waits for them, and re-layouts: 2.88 us -> 1.39 us
  Pallas kernels: 20.2 us -> 21.2 us
    unnamed x4 -> x8, local copies, waits for them, and re-layouts: 2.88 us -> 1.39 us
    pallas_call x0 -> x1, Pallas kernels: none -> 1.25 us  [per_device(): pl.pallas_call(functools.partial(update_kernel, chunk), out_shape=(jax.Sh...]
    pallas_call x1, Pallas kernels: 20.2 us -> 19.9 us  [per_device(): pl.pallas_call(functools.partial(kernel, groups, lanes), out_shape=(jax.S...]
where the time goes in v2:
time: 23.5 us; the launch traced here: 23.2 us
  Pallas kernels  21.2 us (90%)
  local copies, waits for them, and re-layouts  1.39 us (6%)
  between operations  0.67 us (3%)
    pallas_call x1, Pallas kernels, per_device(): pl.pallas_call(functools.partial(kernel, groups, lanes), out_shape=(jax.S...  19.9 us
    unnamed x8, local copies, waits for them, and re-layouts  1.39 us
    pallas_call x1, Pallas kernels, per_device(): pl.pallas_call(functools.partial(update_kernel, chunk), out_shape=(jax.Sh...  1.25 us

profile of v2, /device:TPU:0, one launch (start us, length us, event | category | flops | bytes accessed | tf_op | source)
XLA Modules:
  0.0 23.2 jit_solution(9604540455710754196)
XLA Ops:
  0.6 0.0 copy-start
  0.6 19.9 %shard_map.77 = (bf16[32,256]{1,0:T(8,128)(2,1)}, f32[1,32]{1,0:T(1,128)}, f32[4,256]{1,0:T(4,128)}) custom-call(bf16[2048,256]{1,0:T(8,128)(2,1)} %bitcast.6, s32[16,128]{1,0:T(8,128)} %bitcast.8, s32[4,8,512]{2,1,0:T(8,128)} %bitcast.7, s32[2,8]{1,0:T(2,128)} %bitcast.9, f32[4,256]{1,0:T(4,128)} %accum_hbm.1), custom_call_target="tpu_custom_call" | custom-call | flops 67108864 | bytes 16777216 | tf_op jit(solution)/shard_map/pallas_call | solution.py:333
  20.6 0.0 copy-start.2
  20.6 0.0 copy-start.3
  20.6 0.0 copy-done
  20.6 0.7 %copy-done.2 = f32[4,256]{1,0:T(4,128)S(1)} copy-done((f32[4,256]{1,0:T(4,128)S(1)}, f32[4,256]{1,0:T(4,128)}, u32[]{:S(2)}) %copy-start.2) | copy-done | bytes 4120
  21.3 0.0 copy-done.3
  21.3 0.0 copy-start.1
  21.3 0.7 %copy-done.1 = bf16[32,256]{1,0:T(8,128)(2,1)S(1)} copy-done((bf16[32,256]{1,0:T(8,128)(2,1)S(1)}, bf16[32,256]{1,0:T(8,128)(2,1)}, u32[]{:S(2)}) %copy-start.1) | copy-done | bytes 16408
  22.0 1.3 %shard_map.78 = (f32[4,256,256]{2,1,0:T(8,128)}, f32[4,256]{1,0:T(4,128)}) custom-call(f32[4,256,256]{2,1,0:T(8,128)S(1)} %copy-done, bf16[32,256]{1,0:T(8,128)(2,1)S(1)} %copy-done.1, f32[1,32]{1,0:T(1,128)S(1)} %copy-done.3, f32[4,256]{1,0:T(4,128)S(1)} %copy-done.2), custom_call_target="tpu_custom_call" | custom-call | tf_op jit(solution)/shard_map/pallas_call | solution.py:381
Async XLA Ops:
  0.6 20.0 %copy-start = (f32[4,256,256]{2,1,0:T(8,128)S(1)}, f32[4,256,256]{2,1,0:T(8,128)}, u32[]{:S(2)}) copy-start(f32[4,256,256]{2,1,0:T(8,128)} %weights.1) | copy-start | bytes 3145732
  20.6 0.7 %copy-start.2 = (f32[4,256]{1,0:T(4,128)S(1)}, f32[4,256]{1,0:T(4,128)}, u32[]{:S(2)}) copy-start(f32[4,256]{1,0:T(4,128)} %get-tuple-element.7.accum_any) | copy-start | bytes 12292
  20.6 0.7 %copy-start.3 = (f32[1,32]{1,0:T(1,128)S(1)}, f32[1,32]{1,0:T(1,128)}, u32[]{:S(2)}) copy-start(f32[1,32]{1,0:T(1,128)} %get-tuple-element.6.place_any) | copy-start | bytes 388
  21.3 0.7 %copy-start.1 = (bf16[32,256]{1,0:T(8,128)(2,1)S(1)}, bf16[32,256]{1,0:T(8,128)(2,1)}, u32[]{:S(2)}) copy-start(bf16[32,256]{1,0:T(8,128)(2,1)} %get-tuple-element.5.delta_any) | copy-start | bytes 49156

commit v3 on v2

--- a/solution.py
+++ b/solution.py
@@ -35,19 +35,20 @@
 def kernel(
     groups,
     lanes,
+    place_base,
+    accum_base,
     grad_hbm,
     len_hbm,
     look_hbm,
     slot_hbm,
     accum_hbm,
-    delta_out,
-    place_out,
-    aout,
+    packed,
     grad_in,
     grad_f32,
     grad_t,
     len_v,
     marks,
+    marks_in,
     marks_out,
     slot_v,
     accum_v,
@@ -87,7 +88,7 @@
     def partial_of(m):
         highs, lows = [], []
         for t in range(tables):
-            mark = marks[m, t]
+            mark = marks[m, t].astype(F32)
             count = jnp.zeros((slots, batch), F32)
             for j in range(depth):
                 count += jnp.where(mark[j : j + 1, :] == number, 1.0, 0.0)
@@ -111,20 +112,19 @@
             barrier, inc=1, device_id=(far // lanes, far % lanes), device_id_type=MESH
         )
 
+    look_copies = []
+    for k, step in enumerate(lane_steps):
+        q = lane_peer(step, 1)
+        src = look_hbm.at[:, :, pl.ds(pl.multiple_of(q * batch, batch), batch)]
+        look_copies.append(pltpu.make_async_copy(src, marks_in.at[k], look_sem.at[k]))
+        look_copies[-1].start()
+    grad_copy = pltpu.make_async_copy(grad_hbm, grad_in, load_sem.at[0])
+    grad_copy.start()
     if devices <= 64:
         for i in sorted(range(devices - 1), key=lambda i: abs(i + 1 - devices // 2)):
             greet(i)
     else:
         each(devices - 1, greet)
-    look_copies = []
-    for k, step in enumerate(lane_steps):
-        q = lane_peer(step, 1)
-        src = look_hbm.at[:, :, pl.ds(pl.multiple_of(q * batch, batch), batch)]
-        dst = marks.at[lane] if k == 0 else marks_out.at[k - 1]
-        look_copies.append(pltpu.make_async_copy(src, dst, look_sem.at[k]))
-        look_copies[-1].start()
-    grad_copy = pltpu.make_async_copy(grad_hbm, grad_in, load_sem.at[0])
-    grad_copy.start()
     small_copies = [
         pltpu.make_async_copy(len_hbm, len_v, load_sem.at[1]),
         pltpu.make_async_copy(slot_hbm, slot_v, load_sem.at[2]),
@@ -134,19 +134,8 @@
         copy.start()
     for copy in look_copies:
         copy.wait()
-    grad_copy.wait()
-    for c in range(embed // 128):
-        grad_f32[c] = grad_in[:, c * 128 : (c + 1) * 128].astype(F32)
-    for t in range(tables_all):
-        for c in range(embed // 128):
-            grad_t[t, :, c * 128 : (c + 1) * 128] = grad_f32[
-                c, pl.ds(t, batch, stride=tables_all), :
-            ].astype(BF16)
-    for copy in small_copies:
-        copy.wait()
-
-    number = iota((slots, batch), 0)
-    own_part = partial_of(lane)
+    for k in range(1, lanes):
+        marks_out[k - 1] = marks_in[k].astype(F32).astype(marks_out.dtype)
     pl.semaphore_wait(barrier, devices - 1)
 
     a_copies = []
@@ -162,13 +151,26 @@
         copy.start()
         a_copies.append(copy)
 
+    grad_copy.wait()
+    for c in range(embed // 128):
+        grad_f32[c] = grad_in[:, c * 128 : (c + 1) * 128].astype(F32)
+    for t in range(tables_all):
+        for c in range(embed // 128):
+            grad_t[t, :, c * 128 : (c + 1) * 128] = grad_f32[
+                c, pl.ds(t, batch, stride=tables_all), :
+            ].astype(BF16)
+    for copy in small_copies:
+        copy.wait()
+
+    marks[lane] = marks_in[0].astype(F32).astype(marks.dtype)
+    number = iota((slots, batch), 0).astype(F32)
     far_first = sorted(range(groups), key=lambda d: abs(d - groups // 2))
 
     for k, step in enumerate(lane_steps):
         m = lane_peer(step, -1)
         if k > 0:
             a_copies[k - 1].wait_recv()
-        total = own_part if k == 0 else partial_of(m)
+        total = partial_of(m)
         for p in range(groups):
             part[m, p] = total[p * per_peer : (p + 1) * per_peer].astype(BF16)
 
@@ -208,7 +210,7 @@
     first_col = jnp.sum(jnp.where(same & (j_id < i_id), 1.0, 0.0), axis=1, keepdims=True) == 0.0
     first_row = jnp.sum(jnp.where(same & (i_id < j_id), 1.0, 0.0), axis=0, keepdims=True) == 0.0
     place_row = jnp.where(first_row, target_row, -1.0)
-    place_out[...] = jnp.concatenate([place_row, place_row], axis=1)
+    packed[place_base : place_base + 1, :slots] = place_row
     same_w = jnp.where(same, 1.0, 0.0).astype(BF16)
 
     hits = []
@@ -262,51 +264,33 @@
     clip_limit = 0.5 * math.sqrt(devices * slots * embed)
     clip = clip_limit / jnp.maximum(jnp.sqrt(norm_total), clip_limit)
     for t in range(tables):
-        aout[t : t + 1, :] = accum_v[t : t + 1, :] + clip * clip * square_rows[t]
+        packed[accum_base + t : accum_base + t + 1, :rows] = accum_v[t : t + 1, :] + clip * clip * square_rows[t]
     new_accum_col = accum_col + clip * clip * square_col
     delta = LEARN_RATE * clip * grads / (jnp.sqrt(new_accum_col) + EPSILON)
-    delta_high = delta.astype(BF16)
-    delta_out[:slots] = delta_high
-    delta_out[slots:] = (delta - delta_high.astype(F32)).astype(BF16)
+    packed[:slots, :embed] = delta
     told = norm_in.at[pl.ds(0, devices - 1)]
     pltpu.make_async_copy(told, told, c_send).wait()
 
 
 def update_kernel(
-    chunk,
-    weights,
-    delta_any,
-    place_any,
-    accum_any,
-    wout,
-    aout,
-    held,
-    delta,
-    place_row,
-    accum,
-    sems,
-    in_sems,
-    accum_sem,
+    chunk, slots, place_base, accum_base, weights, packed, wout, aout, held, accum, sems, accum_sem
 ):
-    loads = [
-        pltpu.make_async_copy(place_any, place_row, in_sems.at[0]),
-        pltpu.make_async_copy(delta_any, delta, in_sems.at[1]),
-        pltpu.make_async_copy(accum_any, accum, in_sems.at[2]),
-    ]
-    for copy in loads:
-        copy.start()
-    for copy in loads:
-        copy.wait()
+    accum[...] = packed[accum_base : accum_base + accum.shape[0], : accum.shape[1]]
     accum_copy = pltpu.make_async_copy(accum, aout, accum_sem)
     accum_copy.start()
+    delta = packed[:slots, : weights.shape[2]]
+    high = delta.astype(BF16)
+    deltas = jnp.concatenate([high, (delta - high.astype(F32)).astype(BF16)], axis=0)
+    place_row = packed[place_base : place_base + 1, :slots]
+    place_row = jnp.concatenate([place_row, place_row], axis=1)
     tables, rows = weights.shape[0], weights.shape[1]
     copies = []
     for t in range(tables):
         for c in range(0, rows, chunk):
             row_id = (iota((chunk, 1), 0) + (t * rows + c)).astype(F32)
-            place = jnp.where(row_id == place_row[...], 1.0, 0.0).astype(BF16)
+            place = jnp.where(row_id == place_row, 1.0, 0.0).astype(BF16)
             held[t, c : c + chunk] = weights[t, c : c + chunk] - jnp.dot(
-                place, delta[...], preferred_element_type=F32
+                place, deltas, preferred_element_type=F32
             )
             copies.append(
                 pltpu.make_async_copy(
@@ -328,17 +312,17 @@
     per_peer = slot_row.shape[3]
     devices = groups * lanes
     slots = groups * per_peer
+    mark_type = BF16 if slots <= 256 else F32
+    place_base = -(-slots // 8) * 8
+    accum_base = place_base + 8
+    packed_shape = (accum_base + -(-tables // 8) * 8, max(embed, rows, slots))
     anywhere = pl.BlockSpec(memory_space=pl.ANY)
     vmem = pl.BlockSpec(memory_space=pltpu.VMEM)
-    delta, place_row, accum_new = pl.pallas_call(
-        functools.partial(kernel, groups, lanes),
-        out_shape=(
-            jax.ShapeDtypeStruct((2 * slots, embed), BF16),
-            jax.ShapeDtypeStruct((1, 2 * slots), F32),
-            jax.ShapeDtypeStruct(accum.shape, F32),
-        ),
+    packed = pl.pallas_call(
+        functools.partial(kernel, groups, lanes, place_base, accum_base),
+        out_shape=jax.ShapeDtypeStruct(packed_shape, F32),
         in_specs=[pl.BlockSpec(memory_space=pltpu.HBM)] * 5,
-        out_specs=(vmem, vmem, vmem),
+        out_specs=vmem,
         cost_estimate=pl.CostEstimate(
             flops=8 * slots * batch * tables_all * embed,
             bytes_accessed=32 * batch * tables_all * embed,
@@ -349,8 +333,9 @@
             pltpu.VMEM((embed // 128, batch * tables_all, 128), F32),
             pltpu.VMEM((tables_all, batch, embed), BF16),
             pltpu.VMEM((tables_all, batch), jnp.int32),
+            pltpu.VMEM((lanes, tables, depth, batch), mark_type),
             pltpu.VMEM((lanes, tables, depth, batch), jnp.int32),
-            pltpu.VMEM((lanes - 1, tables, depth, batch), jnp.int32),
+            pltpu.VMEM((lanes - 1, tables, depth, batch), mark_type),
             pltpu.VMEM((per_peer, groups), jnp.int32),
             pltpu.VMEM((tables, rows), F32),
             pltpu.VMEM((lanes, groups, per_peer, embed), BF16),
@@ -379,24 +364,21 @@
     )
     chunk = min(rows, 128)
     return pl.pallas_call(
-        functools.partial(update_kernel, chunk),
+        functools.partial(update_kernel, chunk, slots, place_base, accum_base),
         out_shape=(
             jax.ShapeDtypeStruct(weights.shape, F32),
             jax.ShapeDtypeStruct(accum.shape, F32),
         ),
-        in_specs=[vmem, anywhere, anywhere, anywhere],
+        in_specs=[vmem, vmem],
         out_specs=(anywhere, anywhere),
         scratch_shapes=[
             pltpu.VMEM(weights.shape, F32),
-            pltpu.VMEM(delta.shape, BF16),
-            pltpu.VMEM(place_row.shape, F32),
             pltpu.VMEM(accum.shape, F32),
             pltpu.SemaphoreType.DMA((tables * (rows // chunk),)),
-            pltpu.SemaphoreType.DMA((3,)),
             pltpu.SemaphoreType.DMA,
         ],
         compiler_params=pltpu.CompilerParams(vmem_limit_bytes=8 << 20),
-    )(weights, delta, place_row, accum_new)
+    )(weights, packed)
 
 
 def solution(mesh):

time: 23.5 us -> 22.7 us (0.966)
  local copies, waits for them, and re-layouts: 1.39 us -> 0.76 us
    unnamed x8 -> x4, local copies, waits for them, and re-layouts: 1.39 us -> 0.76 us
where the time goes in v3:
time: 22.7 us; the launch traced here: 22.5 us
  Pallas kernels  21.1 us (93%)
  local copies, waits for them, and re-layouts  0.76 us (3%)
  between operations  0.66 us (3%)
    pallas_call x1, Pallas kernels, per_device(): pl.pallas_call(functools.partial(kernel, groups, lanes, place_base, accum...  19.8 us
    pallas_call x1, Pallas kernels, per_device(): pl.pallas_call(functools.partial(update_kernel, chunk, slots, place_base,...  1.28 us
    unnamed x4, local copies, waits for them, and re-layouts  0.76 us

profile of v3, /device:TPU:0, one launch (start us, length us, event | category | flops | bytes accessed | tf_op | source)
XLA Modules:
  0.0 22.5 jit_solution(13624028841417087788)
XLA Ops:
  0.6 0.0 copy-start
  0.6 19.8 %shard_map.77.packed = f32[32,256]{1,0:T(8,128)} custom-call(bf16[2048,256]{1,0:T(8,128)(2,1)} %bitcast.6, s32[16,128]{1,0:T(8,128)} %bitcast.8, s32[4,8,512]{2,1,0:T(8,128)} %bitcast.7, s32[2,8]{1,0:T(2,128)} %bitcast.9, f32[4,256]{1,0:T(4,128)} %accum_hbm.1), custom_call_target="tpu_custom_call" | custom-call | flops 67108864 | bytes 16777216 | tf_op jit(solution)/shard_map/pallas_call | solution.py:321
  20.5 0.0 copy-done
  20.5 0.0 copy-start.1
  20.5 0.7 %copy-done.1 = f32[32,256]{1,0:T(8,128)S(1)} copy-done((f32[32,256]{1,0:T(8,128)S(1)}, f32[32,256]{1,0:T(8,128)}, u32[]{:S(2)}) %copy-start.1) | copy-done | bytes 32792
  21.3 1.3 %shard_map.78 = (f32[4,256,256]{2,1,0:T(8,128)}, f32[4,256]{1,0:T(4,128)}) custom-call(f32[4,256,256]{2,1,0:T(8,128)S(1)} %copy-done, f32[32,256]{1,0:T(8,128)S(1)} %copy-done.1), custom_call_target="tpu_custom_call" | custom-call | tf_op jit(solution)/shard_map/pallas_call | solution.py:366
Async XLA Ops:
  0.6 19.9 %copy-start = (f32[4,256,256]{2,1,0:T(8,128)S(1)}, f32[4,256,256]{2,1,0:T(8,128)}, u32[]{:S(2)}) copy-start(f32[4,256,256]{2,1,0:T(8,128)} %weights.1) | copy-start | bytes 3145732
  20.5 0.8 %copy-start.1 = (f32[32,256]{1,0:T(8,128)S(1)}, f32[32,256]{1,0:T(8,128)}, u32[]{:S(2)}) copy-start(f32[32,256]{1,0:T(8,128)} %shard_map.77.packed) | copy-start | bytes 98308

commit v4 on v3

--- a/solution.py
+++ b/solution.py
@@ -76,6 +76,7 @@
     grp = lax.axis_index("grp")
     lane = lax.axis_index("lane")
     me = grp * lanes + lane
+    sign = 2 * (grp // (groups // 2)) - 1
 
     lane_steps = [(dx, dc) for dx in range(lanes // 2) for dc in range(2)]
 
@@ -107,7 +108,7 @@
     barrier = pltpu.get_barrier_semaphore()
 
     def greet(i):
-        far = (me + i + 1) % devices
+        far = (me + sign * (i + 1) + devices) % devices
         pl.semaphore_signal(
             barrier, inc=1, device_id=(far // lanes, far % lanes), device_id_type=MESH
         )
@@ -121,7 +122,7 @@
     grad_copy = pltpu.make_async_copy(grad_hbm, grad_in, load_sem.at[0])
     grad_copy.start()
     if devices <= 64:
-        for i in sorted(range(devices - 1), key=lambda i: abs(i + 1 - devices // 2)):
+        for i in range(devices - 1):
             greet(i)
     else:
         each(devices - 1, greet)
@@ -164,7 +165,7 @@
 
     marks[lane] = marks_in[0].astype(F32).astype(marks.dtype)
     number = iota((slots, batch), 0).astype(F32)
-    far_first = sorted(range(groups), key=lambda d: abs(d - groups // 2))
+    far_first = list(range(1, groups)) + [0]
 
     for k, step in enumerate(lane_steps):
         m = lane_peer(step, -1)
@@ -189,7 +190,7 @@
                 if k == 0 and dp == 0:
                     pltpu.make_async_copy(part.at[m, grp], recv.at[me], b_recv).start()
                 else:
-                    send((grp + dp) % groups)
+                    send((grp + sign * dp + groups) % groups)
         else:
             each(groups - 1, lambda i: send((grp + i + 1) % groups))
             if k == 0:
@@ -245,8 +246,8 @@
         ).start()
 
     if devices <= 64:
-        for d in sorted(range(1, devices), key=lambda d: abs(d - devices // 2)):
-            tell((me + d) % devices)
+        for d in range(1, devices):
+            tell((me + sign * d + devices) % devices)
     else:
         each(devices - 1, lambda i: tell((me + i + 1) % devices))
     pltpu.make_async_copy(norm_out, norm_in.at[me], c_recv).start()

time: 22.7 us -> 22.2 us (0.978)
  Pallas kernels: 21.1 us -> 20.6 us
    pallas_call x1, Pallas kernels: 19.8 us -> 19.3 us  [per_device(): pl.pallas_call(functools.partial(kernel, groups, lanes, place_base, accum...]
where the time goes in v4:
time: 22.2 us; the launch traced here: 22 us
  Pallas kernels  20.6 us (93%)
  local copies, waits for them, and re-layouts  0.76 us (3%)
  between operations  0.66 us (3%)
    pallas_call x1, Pallas kernels, per_device(): pl.pallas_call(functools.partial(kernel, groups, lanes, place_base, accum...  19.3 us
    pallas_call x1, Pallas kernels, per_device(): pl.pallas_call(functools.partial(update_kernel, chunk, slots, place_base,...  1.28 us
    unnamed x4, local copies, waits for them, and re-layouts  0.76 us

profile of v4, /device:TPU:0, one launch (start us, length us, event | category | flops | bytes accessed | tf_op | source)
XLA Modules:
  0.0 22.0 jit_solution(12949965207628892534)
XLA Ops:
  0.6 0.0 copy-start
  0.6 19.3 %shard_map.77.packed = f32[32,256]{1,0:T(8,128)} custom-call(bf16[2048,256]{1,0:T(8,128)(2,1)} %bitcast.6, s32[16,128]{1,0:T(8,128)} %bitcast.8, s32[4,8,512]{2,1,0:T(8,128)} %bitcast.7, s32[2,8]{1,0:T(2,128)} %bitcast.9, f32[4,256]{1,0:T(4,128)} %accum_hbm.1), custom_call_target="tpu_custom_call" | custom-call | flops 67108864 | bytes 16777216 | tf_op jit(solution)/shard_map/pallas_call | solution.py:322
  19.9 0.0 copy-done
  20.0 0.0 copy-start.1
  20.0 0.7 %copy-done.1 = f32[32,256]{1,0:T(8,128)S(1)} copy-done((f32[32,256]{1,0:T(8,128)S(1)}, f32[32,256]{1,0:T(8,128)}, u32[]{:S(2)}) %copy-start.1) | copy-done | bytes 32792
  20.7 1.3 %shard_map.78 = (f32[4,256,256]{2,1,0:T(8,128)}, f32[4,256]{1,0:T(4,128)}) custom-call(f32[4,256,256]{2,1,0:T(8,128)S(1)} %copy-done, f32[32,256]{1,0:T(8,128)S(1)} %copy-done.1), custom_call_target="tpu_custom_call" | custom-call | tf_op jit(solution)/shard_map/pallas_call | solution.py:367
Async XLA Ops:
  0.6 19.3 %copy-start = (f32[4,256,256]{2,1,0:T(8,128)S(1)}, f32[4,256,256]{2,1,0:T(8,128)}, u32[]{:S(2)}) copy-start(f32[4,256,256]{2,1,0:T(8,128)} %weights.1) | copy-start | bytes 3145732
  20.0 0.8 %copy-start.1 = (f32[32,256]{1,0:T(8,128)S(1)}, f32[32,256]{1,0:T(8,128)}, u32[]{:S(2)}) copy-start(f32[32,256]{1,0:T(8,128)} %shard_map.77.packed) | copy-start | bytes 98308
